TPU v7x, 128 devices: a whole 4x4x4 slice. The times are simulated.
128 devices in a mesh: row: 16 (over y, x), col: 4 (over z), depth: 2 (over core).
Axes of the slice: x: 4, y: 4, z: 4, core: 2. Of those that a mesh axis runs over, the one named last changes fastest.
Arguments:
- layers: float32 [2, 16384, 16384], P('depth', 'row', 'col'), may hold values from -3 to 265.4, as said below
Outputs:
- factor: float32 [2, 16384, 512], P(None, 'row', 'depth')
- schur: float32 [16384, 16384], P(('row', 'depth'), 'col')
Inputs may be any that keep to these rules, and one draw needn't show every extreme that they name: Read in matrix order, each layer is symmetric, and the sum over layers is symmetric positive definite with a diagonal of order sqrt(16384).
All inputs are finite; a program needn't handle non-finite values.
Results may differ from a plain program's by a relative error of at most 0.0001.
Values sent between devices are 32-bit elements; how exact they have to be, the bound alone decides.
No kernel may reach another device: no remote copies, remote signals or barrier semaphores. Data moves between devices by JAX's collectives and lax.ppermute only.
A program may use at most 192 MiB of HBM per device.

v0:
```python
import jax
import jax.numpy as jnp
from jax import lax
from jax.sharding import PartitionSpec as P

PANEL = 512
PANELS = 2


def broadcast(value, axis, source):
    kept = jnp.where(lax.axis_index(axis) == source, value, 0).astype(value.dtype)
    return lax.psum(kept, axis)


def sent_to_all(x, axis):
    devices = lax.axis_size(axis)
    return lax.all_to_all(jnp.broadcast_to(x[None], (devices, *x.shape)), axis, 0, 0, tiled=True)


def of_everyone(x, axis):
    return sent_to_all(x, axis).sum(axis=0)


def cut_along(x, dim, devices):
    before, after = (x.shape[:dim], x.shape[dim + 1 :])
    return jnp.moveaxis(x.reshape(*before, devices, -1, *after), dim, 0)


def summed_on_arrival(x, axis, dim):
    devices = lax.axis_size(axis)
    tiles = lax.all_to_all(cut_along(x, dim, devices), axis, 0, 0, tiled=True)
    return jnp.sum(tiles, axis=0)


def broadcast_2(x, axis, root):
    return lax.dynamic_index_in_dim(lax.all_gather(x, axis), root, 0, keepdims=False)


def block_inverse(diagonal, identity_block):
    lower_diag = jnp.linalg.cholesky(diagonal)
    return jax.scipy.linalg.solve_triangular(lower_diag, identity_block, lower=True)


def outer_update(left_rows, right_rows):
    return lax.dot_general(
        left_rows,
        right_rows,
        (((1,), (1,)), ((), ())),
        precision=lax.Precision.HIGHEST,
        preferred_element_type=jnp.float32,
    )


def per_device(layers):
    row_groups = lax.axis_size("row")
    col_groups = lax.axis_size("col")
    depth_groups = lax.axis_size("depth")
    row_index = lax.axis_index("row")
    col_index = lax.axis_index("col")
    depth_index = lax.axis_index("depth")
    layer_part = layers[0]
    rows_local = layer_part.shape[0]
    cols_local = layer_part.shape[1]
    slice_width = PANEL // depth_groups
    quarter_rows = rows_local // depth_groups
    local_blocks = rows_local // PANEL
    row_block = jnp.arange(rows_local, dtype=jnp.int32) // PANEL * row_groups + row_index
    col_block = jnp.arange(cols_local, dtype=jnp.int32) // PANEL * col_groups + col_index
    identity_block = jnp.eye(PANEL, dtype=jnp.float32)
    factor_list = []
    schur = None
    for panel_step in range(PANELS):
        owner_col = panel_step % col_groups
        local_col = panel_step // col_groups
        owner_row = panel_step % row_groups
        local_row = panel_step // row_groups
        column = layer_part[:, local_col * PANEL : (local_col + 1) * PANEL]
        layer_diag = broadcast(
            column[local_row * PANEL : (local_row + 1) * PANEL], "row", owner_row
        )
        diagonal = of_everyone(layer_diag, "depth")
        quarter = summed_on_arrival(column, "depth", 0)
        inverse = block_inverse(diagonal, identity_block)
        solved = jnp.dot(quarter, inverse.T, precision=lax.Precision.HIGHEST)
        quarter_block = lax.dynamic_slice_in_dim(
            row_block, depth_index * quarter_rows, quarter_rows, 0
        )
        solved = jnp.where(quarter_block[:, None] >= panel_step, solved, 0.0)
        row_slice = lax.all_to_all(solved, "depth", split_axis=1, concat_axis=0, tiled=True)
        panel_rows = broadcast_2(row_slice, "col", owner_col)
        factor_list.append(panel_rows)
        update_rows = jnp.where(row_block[:, None] > panel_step, panel_rows, 0.0)
        gathered = lax.all_gather(panel_rows, "row", axis=0, tiled=True)
        grouped = gathered.reshape(
            row_groups // col_groups, col_groups, local_blocks, PANEL, slice_width
        )
        picked = lax.dynamic_index_in_dim(grouped, col_index, 1, keepdims=False)
        column_rows = picked.transpose(1, 0, 2, 3).reshape(cols_local, slice_width)
        update_cols = jnp.where(col_block[:, None] > panel_step, column_rows, 0.0)
        if panel_step + 1 < PANELS:
            layer_part = layer_part - outer_update(update_rows, update_cols)
        else:
            schur = summed_on_arrival(
                layer_part - outer_update(update_rows, update_cols), "depth", 0
            )
    return (jnp.stack(factor_list), schur)


def solution(mesh):
    return jax.shard_map(
        per_device,
        mesh=mesh,
        in_specs=(P("depth", "row", "col"),),
        out_specs=(P(None, "row", "depth"), P(("row", "depth"), "col")),
        check_vma=False,
    )
```

profile of v0, /device:TPU:1, one launch (start us, length us, event | category | flops | bytes accessed | tf_op | source)
XLA Modules:
  0.0 959.5 jit_solution(3367410215411466751)
XLA Ops:
  7.2 17.5 %copy.41 = f32[1,1024,4096]{1,2,0:T(8,128)} copy(f32[1,1024,4096]{2,1,0:T(8,128)} %param.4) | data formatting | bytes 33554432 | tf_op args[0]
  24.7 2.3 slice_select_fusion.1
  27.0 1.7 slice.113
  28.7 1.5 copy.80
  30.2 5.1 all-to-all-start
  35.4 2.5 all-to-all-done
  39.3 76.7 %all-reduce.4.cloned.1.call-done = f32[512,512]{0,1:T(8,128)} async-done(((f32[512,512]{0,1:T(8,128)}), f32[512,512]{0,1:T(8,128)}) %all-reduce.4.cloned.1.call-update) | async-done | bytes 1048592 | tf_op jit(solution)/shard_map/psum | solution.py:12
  116.0 1.6 copy.44
  117.8 8.2 all_to_all.57
  126.0 1.9 reduce_sum.46
  129.4 11.7 %cholesky.286 = f32[128,128]{1,0:T(8,128)S(1)} custom-call(f32[128,128]{1,0:T(8,128)S(1)} %cholesky.426), custom_call_target="Cholesky" | custom-call | tf_op jit(solution)/shard_map/jit(cholesky)/cholesky | solution.py:40
  141.2 9.8 %custom-call.27 = f32[1,128,128]{1,2,0:T(8,128)S(1)} custom-call(f32[1,128,128]{2,1,0:T(8,128)S(1)} %get-tuple-element.63), custom_call_target="InvertDiagBlocksLowerTriangular" | custom-call | tf_op jit(solution)/shard_map/jit(cholesky)/cholesky | solution.py:40
  153.6 11.7 %cholesky.305 = f32[128,128]{1,0:T(8,128)S(1)} custom-call(f32[128,128]{1,0:T(8,128)S(1)} %cholesky.430), custom_call_target="Cholesky" | custom-call | tf_op jit(solution)/shard_map/jit(cholesky)/cholesky | solution.py:40
  165.4 10.1 %custom-call.28 = f32[1,128,128]{1,2,0:T(8,128)S(1)} custom-call(f32[1,128,128]{2,1,0:T(8,128)S(1)} %get-tuple-element.60), custom_call_target="InvertDiagBlocksLowerTriangular" | custom-call | tf_op jit(solution)/shard_map/jit(cholesky)/cholesky | solution.py:40
  177.1 11.7 %cholesky.326 = f32[128,128]{1,0:T(8,128)S(1)} custom-call(f32[128,128]{1,0:T(8,128)S(1)} %cholesky.435), custom_call_target="Cholesky" | custom-call | tf_op jit(solution)/shard_map/jit(cholesky)/cholesky | solution.py:40
  189.5 9.8 %custom-call.29 = f32[1,128,128]{1,2,0:T(8,128)S(1)} custom-call(f32[1,128,128]{2,1,0:T(8,128)S(1)} %get-tuple-element.57), custom_call_target="InvertDiagBlocksLowerTriangular" | custom-call | tf_op jit(solution)/shard_map/jit(cholesky)/cholesky | solution.py:40
  200.7 11.9 %cholesky.343 = f32[128,128]{1,0:T(8,128)S(1)} custom-call(f32[128,128]{1,0:T(8,128)S(1)} %convolution_subtract_fusion.13), custom_call_target="Cholesky" | custom-call | tf_op jit(solution)/shard_map/jit(cholesky)/cholesky | solution.py:40
  217.7 11.7 %while.4 = (s32[]{:T(128)}, f32[512,512]{1,0:T(8,128)}, s32[4,2]{0,1:T(2,128)S(1)}, f32[4,128,128]{2,1,0:T(8,128)S(1)}, s32[]{:T(128)}) while((s32[]{:T(128)}, f32[512,512]{1,0:T(8,128)}, s32[4,2]{0,1:T(2,128)S(1)}, f32[4,128,128]{2,1,0:T(8,128)S(1)}, s32[]{:T(128)}) %tuple.58), condition=%wide.while_cond, body=%wide.while_body.sunk | while | flops 2 | bytes 131181 | solution.py:41
  218.3 2.2 bitcast_dynamic-update-slice_fusion.4
  221.3 2.2 bitcast_dynamic-update-slice_fusion.4
  224.2 2.2 bitcast_dynamic-update-slice_fusion.4
  227.2 2.2 bitcast_dynamic-update-slice_fusion.4
  229.3 39.3 %custom-call.30 = f32[4,128,128]{1,2,0:T(8,128)S(1)} custom-call(f32[4,128,128]{2,1,0:T(8,128)S(1)} %get-tuple-element.18), custom_call_target="InvertDiagBlocksLowerTriangular" | custom-call | tf_op jit(solution)/shard_map/jit(_solve_triangular)/triangular_solve | solution.py:41
  270.7 1.3 convolution_subtract_fusion.4
  272.5 1.6 convolution_subtract_fusion.7
  274.5 1.9 convolution_select_fusion.1
  276.4 4.6 all_to_all.58
  282.4 47.3 %all-gather.7.cloned.1.call-done = f32[4,1024,256]{2,1,0:T(8,128)} async-done(((f32[1,1024,256]{2,1,0:T(8,128)}), f32[4,1024,256]{2,1,0:T(8,128)}) %all-gather.7.cloned.1.call-update) | async-done | bytes 4194320 | tf_op jit(solution)/shard_map/all_gather | solution.py:36
  329.7 2.3 dynamic_slice.23
  332.1 111.6 %all-gather.11.cloned.1.call-done = f32[1,16384,256]{2,1,0:T(8,128)} async-done(((f32[1,1024,256]{2,1,0:T(8,128)}), f32[1,16384,256]{2,1,0:T(8,128)}) %all-gather.11.cloned.1.call-update) | async-done | bytes 16777232 | tf_op jit(solution)/shard_map/all_gather | solution.py:93
  443.7 3.3 fusion.1
  446.9 19.2 %convolution_subtract_fusion.1 = f32[1024,4096]{0,1:T(8,128)} fusion(f32[4096,256]{1,0:T(8,128)S(1)} %bitcast.148, pred[1024]{0:T(1024)(128)(4,1)S(1)} %broadcast_compare_fusion.2, f32[1,1024,4096]{1,2,0:T(8,128)} %copy.41, f32[4,1024,256]{2,1,0:T(8,128)} %all-gather.7.cloned.1.call-done), kind=kOutput, calls=%fused_computation.6 | convolution fusion | flops 12889358336 | bytes 38798336 | tf_op jit(solution)/shard_map/dot_general | solution.py:45
  466.1 2.5 slice_select_fusion
  468.9 5.9 all_to_all.59
  476.0 78.3 %all-reduce.6.cloned.1.call-done = f32[512,512]{0,1:T(8,128)} async-done(((f32[512,512]{0,1:T(8,128)}), f32[512,512]{0,1:T(8,128)}) %all-reduce.6.cloned.1.call-update) | async-done | bytes 1048592 | tf_op jit(solution)/shard_map/psum | solution.py:12
  554.3 1.6 copy.51
  556.1 8.2 all_to_all.60
  564.2 1.9 reduce_sum.48
  567.7 11.7 %cholesky.358 = f32[128,128]{1,0:T(8,128)S(1)} custom-call(f32[128,128]{1,0:T(8,128)S(1)} %cholesky.439), custom_call_target="Cholesky" | custom-call | tf_op jit(solution)/shard_map/jit(cholesky)/cholesky | solution.py:40
  579.6 9.8 %custom-call.31 = f32[1,128,128]{1,2,0:T(8,128)S(1)} custom-call(f32[1,128,128]{2,1,0:T(8,128)S(1)} %get-tuple-element.53), custom_call_target="InvertDiagBlocksLowerTriangular" | custom-call | tf_op jit(solution)/shard_map/jit(cholesky)/cholesky | solution.py:40
  591.9 11.7 %cholesky.377 = f32[128,128]{1,0:T(8,128)S(1)} custom-call(f32[128,128]{1,0:T(8,128)S(1)} %cholesky.443), custom_call_target="Cholesky" | custom-call | tf_op jit(solution)/shard_map/jit(cholesky)/cholesky | solution.py:40
  605.0 10.0 %custom-call.32 = f32[1,128,128]{1,2,0:T(8,128)S(1)} custom-call(f32[1,128,128]{2,1,0:T(8,128)S(1)} %get-tuple-element.50), custom_call_target="InvertDiagBlocksLowerTriangular" | custom-call | tf_op jit(solution)/shard_map/jit(cholesky)/cholesky | solution.py:40
  616.6 11.7 %cholesky.398 = f32[128,128]{1,0:T(8,128)S(1)} custom-call(f32[128,128]{1,0:T(8,128)S(1)} %cholesky.448), custom_call_target="Cholesky" | custom-call | tf_op jit(solution)/shard_map/jit(cholesky)/cholesky | solution.py:40
  629.0 9.8 %custom-call.33 = f32[1,128,128]{1,2,0:T(8,128)S(1)} custom-call(f32[1,128,128]{2,1,0:T(8,128)S(1)} %get-tuple-element.47), custom_call_target="InvertDiagBlocksLowerTriangular" | custom-call | tf_op jit(solution)/shard_map/jit(cholesky)/cholesky | solution.py:40
  640.3 11.9 %cholesky.415 = f32[128,128]{1,0:T(8,128)S(1)} custom-call(f32[128,128]{1,0:T(8,128)S(1)} %convolution_subtract_fusion.12), custom_call_target="Cholesky" | custom-call | tf_op jit(solution)/shard_map/jit(cholesky)/cholesky | solution.py:40
  656.4 11.7 %while.5 = (s32[]{:T(128)}, f32[512,512]{1,0:T(8,128)}, s32[4,2]{0,1:T(2,128)S(1)}, f32[4,128,128]{2,1,0:T(8,128)S(1)}, s32[]{:T(128)}) while((s32[]{:T(128)}, f32[512,512]{1,0:T(8,128)}, s32[4,2]{0,1:T(2,128)S(1)}, f32[4,128,128]{2,1,0:T(8,128)S(1)}, s32[]{:T(128)}) %tuple.76), condition=%wide.while_cond.clone, body=%wide.while_body.clone.sunk | while | flops 2 | bytes 131181 | solution.py:41
  657.1 2.2 bitcast_dynamic-update-slice_fusion.5
  660.1 2.2 bitcast_dynamic-update-slice_fusion.5
  663.0 2.2 bitcast_dynamic-update-slice_fusion.5
  665.9 2.2 bitcast_dynamic-update-slice_fusion.5
  668.1 39.3 %custom-call.34 = f32[4,128,128]{1,2,0:T(8,128)S(1)} custom-call(f32[4,128,128]{2,1,0:T(8,128)S(1)} %get-tuple-element.19), custom_call_target="InvertDiagBlocksLowerTriangular" | custom-call | tf_op jit(solution)/shard_map/jit(_solve_triangular)/triangular_solve | solution.py:41
  711.3 1.6 convolution_subtract_fusion.6
  713.3 1.9 convolution_select_fusion
  715.2 4.7 all_to_all.61
  721.3 47.3 %all-gather.9.cloned.1.call-done = f32[4,1024,256]{2,1,0:T(8,128)} async-done(((f32[1,1024,256]{2,1,0:T(8,128)}), f32[4,1024,256]{2,1,0:T(8,128)}) %all-gather.9.cloned.1.call-update) | async-done | bytes 4194320 | tf_op jit(solution)/shard_map/all_gather | solution.py:36
  768.6 2.3 dynamic_slice.24
  770.9 2.7 pad_maximum_fusion
  773.6 108.8 %all-gather.13.cloned.1.call-done = f32[1,16384,256]{2,1,0:T(8,128)} async-done(((f32[1,1024,256]{2,1,0:T(8,128)}), f32[1,16384,256]{2,1,0:T(8,128)}) %all-gather.13.cloned.1.call-update) | async-done | bytes 16777232 | tf_op jit(solution)/shard_map/all_gather | solution.py:93
  882.4 3.5 fusion
  885.9 19.2 %convolution_subtract_fusion = f32[1024,4096]{0,1:T(8,128)} fusion(f32[1024,4096]{0,1:T(8,128)} %convolution_subtract_fusion.1, f32[4096,256]{1,0:T(8,128)S(1)} %bitcast.147, pred[1024]{0:T(1024)(128)(4,1)S(1)} %broadcast_compare_fusion.3, f32[4,1024,256]{2,1,0:T(8,128)} %all-gather.9.cloned.1.call-done), kind=kOutput, calls=%fused_computation.5 | convolution fusion | flops 12889358336 | bytes 38798336 | tf_op jit(solution)/shard_map/dot_general | solution.py:45
  905.1 6.8 copy.78
  911.9 19.5 %all_to_all.62 = f32[2,512,4096]{1,2,0:T(8,128)} all-to-all(f32[2,512,4096]{1,2,0:T(8,128)S(1)} %bitcast.146), channel_id=1, replica_groups=mesh['row'=16,'col'=4,'depth'=2] {'depth'}, dimensions={0} | all-to-all | bytes 33554432 | tf_op jit(solution)/shard_map/all_to_all | solution.py:31
  931.4 11.9 %reduce_sum.49 = f32[512,4096]{0,1:T(8,128)} reduce(f32[2,512,4096]{1,2,0:T(8,128)} %all_to_all.62, f32[]{:T(128)} %constant.194.clone.1), dimensions={0}, to_apply=%region_14.17 | reduce | flops 2097152 | bytes 25165828 | tf_op jit(solution)/shard_map/reduce_sum | solution.py:32
  943.3 8.9 copy.58
  (110 shorter events, 40.3 us)
Async XLA Ops:
  7.2 108.8 %all-reduce.4.cloned.1.call-start = ((), (), s32[]{:S(2)}) async-start(), calls=%async_computation.7 | async-start | bytes 2097152 | tf_op jit(solution)/shard_map/psum | solution.py:12
  30.2 7.6 all-to-all-start
  35.4 294.3 %all-gather.7.cloned.1.call-start = ((), (), s32[]{:S(2)}) async-start(), calls=%async_computation.8 | async-start | bytes 5242880 | tf_op jit(solution)/shard_map/all_gather | solution.py:36
  128.4 1.0 copy-start.4
  216.5 58.0 %copy-start.1 = (f32[512,512]{0,1:T(8,128)S(1)}, f32[512,512]{0,1:T(8,128)}, u32[]{:S(2)}) copy-start(f32[512,512]{0,1:T(8,128)} %reduce_sum.45) | copy-start | bytes 3145732
  282.3 161.3 %all-gather.11.cloned.1.call-start = ((), (), s32[]{:S(2)}) async-start(), calls=%async_computation.11 | async-start | bytes 17825792 | tf_op jit(solution)/shard_map/all_gather | solution.py:93
  331.9 222.3 %all-reduce.6.cloned.1.call-start = ((), (), s32[]{:S(2)}) async-start(), calls=%async_computation.9 | async-start | bytes 2097152 | tf_op jit(solution)/shard_map/psum | solution.py:12
  466.1 2.6 slice-start
  468.6 300.0 %all-gather.9.cloned.1.call-start = ((), (), s32[]{:S(2)}) async-start(), calls=%async_computation.10 | async-start | bytes 5242880 | tf_op jit(solution)/shard_map/all_gather | solution.py:36
  566.7 1.0 copy-start.3
  655.3 58.0 %copy-start.2 = (f32[512,512]{0,1:T(8,128)S(1)}, f32[512,512]{0,1:T(8,128)}, u32[]{:S(2)}) copy-start(f32[512,512]{0,1:T(8,128)} %reduce_sum.47) | copy-start | bytes 3145732
  715.2 55.7 %copy-start = (f32[1,1024,256]{2,1,0:T(8,128)S(1)}, f32[1,1024,256]{2,1,0:T(8,128)}, u32[]{:S(2)}) copy-start(f32[1,1024,256]{2,1,0:T(8,128)} %dynamic_slice.23) | copy-start | bytes 3145732
  721.2 161.2 %all-gather.13.cloned.1.call-start = ((), (), s32[]{:S(2)}) async-start(), calls=%async_computation.12 | async-start | bytes 17825792 | tf_op jit(solution)/shard_map/all_gather | solution.py:93
Sparse Core Ops, SparseCore 0:
  27.1 88.8 all-reduce.3
  282.5 47.1 all-gather.6
  332.4 111.2 all-gather.10
  468.7 85.4 all-reduce.5
  721.4 47.1 all-gather.8
  771.1 111.2 all-gather.12
where the time goes:
time: 972 us; the launch traced here: 960 us
  waiting for transfers between devices  473 us (49%)
  other arithmetic  272 us (28%)
  local copies, waits for them, and re-layouts  73.5 us (8%)
  matrix products  64.6 us (7%)
  blocking collectives  51 us (5%)
  between operations  20.1 us (2%)
    all_gather x2, waiting for transfers between devices, per_device(): gathered = lax.all_gather(panel_rows, 'row', axis=0, tiled=True)  220 us
    another operation x29, other arithmetic, block_inverse(): lower_diag = jnp.linalg.cholesky(diagonal)  158 us
    psum x2, waiting for transfers between devices, broadcast(): return lax.psum(kept, axis)  155 us
    all_gather x2, waiting for transfers between devices, broadcast_2(): lax.all_gather(x, axis)  94.5 us
    another operation x5, other arithmetic, block_inverse(): jax.scipy.linalg.solve_triangular(lower_diag, identity_block, lower=True)  80.9 us
    dot_general x2, matrix products, outer_update(): lax.dot_general(left_rows, right_rows, (((1,), (1,)), ((), ())), precisio...  38.3 us
    unnamed x12, local copies, waits for them, and re-layouts  28.3 us
    all_to_all x2, blocking collectives, summed_on_arrival(): tiles = lax.all_to_all(cut_along(x, dim, devices), axis, 0, 0, tiled=True)  25.4 us
  transfers between devices with their start and end apart: 7, of which 7 were waited for; matrix products, arithmetic and copies ran while one was open for 1% of the time, Pallas kernels for 0%

commit v1 on v0

--- a/solution.py
+++ b/solution.py
@@ -90,7 +90,9 @@
         panel_rows = broadcast_2(row_slice, "col", owner_col)
         factor_list.append(panel_rows)
         update_rows = jnp.where(row_block[:, None] > panel_step, panel_rows, 0.0)
-        gathered = lax.all_gather(panel_rows, "row", axis=0, tiled=True)
+        gathered = jnp.concatenate(
+            lax.all_to_all(jnp.stack([panel_rows] * lax.axis_size("row")), "row", 0, 0), axis=0
+        )
         grouped = gathered.reshape(
             row_groups // col_groups, col_groups, local_blocks, PANEL, slice_width
         )

time: 972 us -> 1280 us (1.32)
  waiting for transfers between devices: 473 us -> 745 us
  local copies, waits for them, and re-layouts: 73.5 us -> 87.9 us
  starting transfers between devices: 5.34 us -> 18.8 us
    all_to_all x0 -> x2, waiting for transfers between devices: none -> 495 us  [per_device(): lax.all_to_all(jnp.stack([panel_rows] * lax.axis_size('row')), 'row', 0, 0)]
    all_gather x2 -> x0, waiting for transfers between devices: 220 us -> none  [per_device(): gathered = lax.all_gather(panel_rows, 'row', axis=0, tiled=True)]
    another operation x0 -> x2, local copies, waits for them, and re-layouts: none -> 14.6 us  [per_device(): jnp.stack([panel_rows] * lax.axis_size('row'))]
    all_to_all x0 -> x2, starting transfers between devices: none -> 13.6 us  [per_device(): lax.all_to_all(jnp.stack([panel_rows] * lax.axis_size('row')), 'row', 0, 0)]
where the time goes in v1:
time: 1280 us; the launch traced here: 1270 us
  waiting for transfers between devices  745 us (58%)
  other arithmetic  281 us (22%)
  local copies, waits for them, and re-layouts  87.9 us (7%)
  matrix products  64.6 us (5%)
  blocking collectives  53.1 us (4%)
  between operations  19.8 us (2%)
  starting transfers between devices  18.8 us (1%)
    all_to_all x2, waiting for transfers between devices, per_device(): lax.all_to_all(jnp.stack([panel_rows] * lax.axis_size('row')), 'row', 0, 0)  495 us
    another operation x29, other arithmetic, block_inverse(): lower_diag = jnp.linalg.cholesky(diagonal)  168 us
    psum x2, waiting for transfers between devices, broadcast(): return lax.psum(kept, axis)  153 us
    all_gather x2, waiting for transfers between devices, broadcast_2(): lax.all_gather(x, axis)  94.7 us
    another operation x5, other arithmetic, block_inverse(): jax.scipy.linalg.solve_triangular(lower_diag, identity_block, lower=True)  80.9 us
    dot_general x2, matrix products, outer_update(): lax.dot_general(left_rows, right_rows, (((1,), (1,)), ((), ())), precisio...  38.3 us
    unnamed x12, local copies, waits for them, and re-layouts  28.3 us
    all_to_all x2, blocking collectives, summed_on_arrival(): tiles = lax.all_to_all(cut_along(x, dim, devices), axis, 0, 0, tiled=True)  27.6 us
  transfers between devices with their start and end apart: 7, of which 7 were waited for; matrix products, arithmetic and copies ran while one was open for 1% of the time, Pallas kernels for 0%

profile of v1, /device:TPU:1, one launch (start us, length us, event | category | flops | bytes accessed | tf_op | source)
XLA Modules:
  0.0 1269.8 jit_solution(5869491338663105507)
XLA Ops:
  7.2 17.5 %copy.60 = f32[1,1024,4096]{1,2,0:T(8,128)} copy(f32[1,1024,4096]{2,1,0:T(8,128)} %param.4) | data formatting | bytes 33554432 | tf_op args[0]
  24.7 2.3 slice_select_fusion.1
  27.0 1.7 slice.113
  30.2 5.1 all-to-all-start
  35.4 2.5 all-to-all-done
  39.3 76.7 %all-reduce.4.cloned.1.call-done = f32[512,512]{0,1:T(8,128)} async-done(((f32[512,512]{0,1:T(8,128)}), f32[512,512]{0,1:T(8,128)}) %all-reduce.4.cloned.1.call-update) | async-done | bytes 1048592 | tf_op jit(solution)/shard_map/psum | solution.py:12
  116.0 1.6 copy.63
  117.8 8.2 all_to_all.67
  126.0 1.9 reduce_sum.46
  129.4 11.7 cholesky.286
  141.2 9.8 custom-call.27
  153.6 11.7 cholesky.305
  165.4 10.0 custom-call.28
  177.0 11.7 cholesky.326
  189.4 9.8 custom-call.29
  200.6 21.9 %cholesky.343 = f32[128,128]{1,0:T(8,128)S(1)} custom-call(f32[128,128]{1,0:T(8,128)S(1)} %convolution_subtract_fusion.13), custom_call_target="Cholesky" | custom-call | tf_op jit(solution)/shard_map/jit(cholesky)/cholesky | solution.py:40
  227.7 11.7 while.4
  228.3 2.2 bitcast_dynamic-update-slice_fusion.4
  231.3 2.2 bitcast_dynamic-update-slice_fusion.4
  234.2 2.2 bitcast_dynamic-update-slice_fusion.4
  237.1 2.2 bitcast_dynamic-update-slice_fusion.4
  239.3 39.3 %custom-call.30 = f32[4,128,128]{1,2,0:T(8,128)S(1)} custom-call(f32[4,128,128]{2,1,0:T(8,128)S(1)} %get-tuple-element.18), custom_call_target="InvertDiagBlocksLowerTriangular" | custom-call | tf_op jit(solution)/shard_map/jit(_solve_triangular)/triangular_solve | solution.py:41
  282.5 1.6 convolution_subtract_fusion.7
  284.5 1.9 convolution_select_fusion.1
  286.4 4.6 all_to_all.68
  292.3 47.3 %all-gather.3.cloned.1.call-done = f32[4,1024,256]{2,1,0:T(8,128)} async-done(((f32[1,1024,256]{2,1,0:T(8,128)}), f32[4,1024,256]{2,1,0:T(8,128)}) %all-gather.3.cloned.1.call-update) | async-done | bytes 4194320 | tf_op jit(solution)/shard_map/all_gather | solution.py:36
  339.7 2.3 fusion.96
  342.0 7.3 stack.6
  349.3 6.6 all-to-all-start.3
  356.0 248.1 %all-to-all-done.3 = f32[16,1024,256]{2,1,0:T(8,128)} async-done(((f32[16,1024,256]{2,1,0:T(8,128)}), f32[16,1024,256]{2,1,0:T(8,128)}, u32[]{:S(2)}, u32[]{:S(2)}) %all-to-all-start.3) | async-done | bytes 16777248 | tf_op jit(solution)/shard_map/all_to_all | solution.py:94
  604.2 3.3 bitcast_select_fusion.1
  607.7 19.2 %convolution_subtract_fusion.1 = f32[1024,4096]{0,1:T(8,128)} fusion(f32[4096,256]{1,0:T(8,128)S(1)} %bitcast.147, pred[1024]{0:T(1024)(128)(4,1)S(1)} %broadcast_compare_fusion.2, f32[1,1024,4096]{1,2,0:T(8,128)} %copy.60, f32[4,1024,256]{2,1,0:T(8,128)} %all-gather.3.cloned.1.call-done), kind=kOutput, calls=%fused_computation.6 | convolution fusion | flops 12889358336 | bytes 38798336 | tf_op jit(solution)/shard_map/dot_general | solution.py:45
  626.9 2.5 slice_select_fusion
  629.7 7.0 all_to_all.69
  637.9 75.9 %all-reduce.6.cloned.1.call-done = f32[512,512]{0,1:T(8,128)} async-done(((f32[512,512]{0,1:T(8,128)}), f32[512,512]{0,1:T(8,128)}) %all-reduce.6.cloned.1.call-update) | async-done | bytes 1048592 | tf_op jit(solution)/shard_map/psum | solution.py:12
  713.8 1.6 copy.70
  715.6 8.2 all_to_all.70
  723.8 1.9 reduce_sum.48
  727.2 11.7 cholesky.358
  739.1 9.8 custom-call.31
  751.4 11.7 cholesky.377
  764.5 10.0 custom-call.32
  776.1 11.7 cholesky.398
  788.5 9.8 custom-call.33
  799.8 11.9 cholesky.415
  815.9 11.7 while.5
  816.6 2.2 bitcast_dynamic-update-slice_fusion.5
  819.6 2.2 bitcast_dynamic-update-slice_fusion.5
  822.5 2.2 bitcast_dynamic-update-slice_fusion.5
  825.4 2.2 bitcast_dynamic-update-slice_fusion.5
  827.6 39.3 %custom-call.34 = f32[4,128,128]{1,2,0:T(8,128)S(1)} custom-call(f32[4,128,128]{2,1,0:T(8,128)S(1)} %get-tuple-element.19), custom_call_target="InvertDiagBlocksLowerTriangular" | custom-call | tf_op jit(solution)/shard_map/jit(_solve_triangular)/triangular_solve | solution.py:41
  870.8 1.6 convolution_subtract_fusion.6
  872.8 1.9 convolution_select_fusion
  874.7 4.6 all_to_all.71
  880.6 47.3 %all-gather.5.cloned.1.call-done = f32[4,1024,256]{2,1,0:T(8,128)} async-done(((f32[1,1024,256]{2,1,0:T(8,128)}), f32[4,1024,256]{2,1,0:T(8,128)}) %all-gather.5.cloned.1.call-update) | async-done | bytes 4194320 | tf_op jit(solution)/shard_map/all_gather | solution.py:36
  929.3 7.3 stack.8
  936.6 7.0 all-to-all-start.7
  945.1 246.8 %all-to-all-done.7 = f32[16,1024,256]{2,1,0:T(8,128)} async-done(((f32[16,1024,256]{2,1,0:T(8,128)}), f32[16,1024,256]{2,1,0:T(8,128)}, u32[]{:S(2)}, u32[]{:S(2)}) %all-to-all-start.7) | async-done | bytes 16777248 | tf_op jit(solution)/shard_map/all_to_all | solution.py:94
  1191.9 3.3 bitcast_select_fusion
  1195.5 19.2 %convolution_subtract_fusion = f32[1024,4096]{0,1:T(8,128)} fusion(f32[1024,4096]{0,1:T(8,128)} %convolution_subtract_fusion.1, f32[4096,256]{1,0:T(8,128)S(1)} %bitcast.148, pred[1024]{0:T(1024)(128)(4,1)S(1)} %broadcast_compare_fusion.3, f32[4,1024,256]{2,1,0:T(8,128)} %all-gather.5.cloned.1.call-done), kind=kOutput, calls=%fused_computation.5 | convolution fusion | flops 12889358336 | bytes 38798336 | tf_op jit(solution)/shard_map/dot_general | solution.py:45
  1214.6 6.8 copy.89
  1221.5 20.6 %all_to_all.72 = f32[2,512,4096]{1,2,0:T(8,128)} all-to-all(f32[2,512,4096]{1,2,0:T(8,128)S(1)} %bitcast.146), channel_id=1, replica_groups=mesh['row'=16,'col'=4,'depth'=2] {'depth'}, dimensions={0} | all-to-all | bytes 33554432 | tf_op jit(solution)/shard_map/all_to_all | solution.py:31
  1242.1 11.9 reduce_sum.49
  1254.0 8.9 copy.77
  (112 shorter events, 46.5 us)
Async XLA Ops:
  7.2 108.8 %all-reduce.4.cloned.1.call-start = ((), (), s32[]{:S(2)}) async-start(), calls=%async_computation.9 | async-start | bytes 2097152 | tf_op jit(solution)/shard_map/psum | solution.py:12
  30.2 7.6 all-to-all-start
  35.4 304.3 %all-gather.3.cloned.1.call-start = ((), (), s32[]{:S(2)}) async-start(), calls=%async_computation.10 | async-start | bytes 5242880 | tf_op jit(solution)/shard_map/all_gather | solution.py:36
  128.4 1.0 copy-start.4
  226.5 58.0 %copy-start.1 = (f32[512,512]{0,1:T(8,128)S(1)}, f32[512,512]{0,1:T(8,128)}, u32[]{:S(2)}) copy-start(f32[512,512]{0,1:T(8,128)} %reduce_sum.45) | copy-start | bytes 3145732
  349.3 254.9 %all-to-all-start.3 = ((f32[16,1024,256]{2,1,0:T(8,128)}), f32[16,1024,256]{2,1,0:T(8,128)}, u32[]{:S(2)}, u32[]{:S(2)}) async-start(f32[16,1024,256]{2,1,0:T(8,128)} %stack.6), calls=%async_computation.3 | async-start | bytes 33554432 | tf_op jit(solution)/shard_map/all_to_all | solution.py:94
  355.9 357.9 %all-reduce.6.cloned.1.call-start = ((), (), s32[]{:S(2)}) async-start(), calls=%async_computation.11 | async-start | bytes 2097152 | tf_op jit(solution)/shard_map/psum | solution.py:12
  626.9 2.6 slice-start
  629.4 298.5 %all-gather.5.cloned.1.call-start = ((), (), s32[]{:S(2)}) async-start(), calls=%async_computation.12 | async-start | bytes 5242880 | tf_op jit(solution)/shard_map/all_gather | solution.py:36
  726.2 1.0 copy-start.3
  814.8 58.0 %copy-start.2 = (f32[512,512]{0,1:T(8,128)S(1)}, f32[512,512]{0,1:T(8,128)}, u32[]{:S(2)}) copy-start(f32[512,512]{0,1:T(8,128)} %reduce_sum.47) | copy-start | bytes 3145732
  936.6 7.1 copy-start
  936.6 255.3 %all-to-all-start.7 = ((f32[16,1024,256]{2,1,0:T(8,128)}), f32[16,1024,256]{2,1,0:T(8,128)}, u32[]{:S(2)}, u32[]{:S(2)}) async-start(f32[16,1024,256]{2,1,0:T(8,128)} %stack.8), calls=%async_computation.7 | async-start | bytes 33554432 | tf_op jit(solution)/shard_map/all_to_all | solution.py:94
Sparse Core Ops, SparseCore 0:
  27.1 88.8 all-reduce.3
  292.4 47.1 all-gather.2
  629.5 84.1 all-reduce.5
  880.7 47.1 all-gather.4
